TPU v7x, 32 devices: a whole 2x2x4 slice. The times are simulated.
32 devices in a mesh: shard: 2 (over x), replica: 16 (over z, y, core).
Axes of the slice: x: 2, y: 2, z: 4, core: 2. Of those that a mesh axis runs over, the one named last changes fastest.
Arguments:
- x_in: bfloat16 [32, 128, 2048], P(('shard', 'replica')), may hold values from -6 to 6
- cotangent: bfloat16 [32, 128, 2048], P(('shard', 'replica')), may hold values from -6 to 6
- w_query: bfloat16 [2048, 1024], P('shard'), may hold values from -0.088388348 to 0.088388348
- w_key: bfloat16 [2048, 1024], P('shard'), may hold values from -0.088388348 to 0.088388348
- w_value: bfloat16 [2048, 1024], P('shard'), may hold values from -0.125 to 0.125
- w_out: bfloat16 [1024, 2048], P('shard'), may hold values from -0.1875 to 0.1875
- w_gate: bfloat16 [2048, 4096], P('shard'), may hold values from -0.125 to 0.125
- w_up: bfloat16 [2048, 4096], P('shard'), may hold values from -0.125 to 0.125
- w_down: bfloat16 [4096, 2048], P('shard'), may hold values from -0.09375 to 0.09375
- gain_query: bfloat16 [1024], P('shard'), may hold values from 0.5 to 5
- gain_key: bfloat16 [1024], P('shard'), may hold values from 0.5 to 5
- gain_attn: bfloat16 [2048], P('shard'), may hold values from 0.5 to 1.5
- gain_mlp: bfloat16 [2048], P('shard'), may hold values from 0.5 to 1.5
Outputs:
- output: bfloat16 [32, 128, 2048], P(('shard', 'replica'))
- grad_input: float32 [32, 128, 2048], P(('shard', 'replica'))
- grad_w_query: float32 [2048, 1024], P(('shard', 'replica'))
- grad_w_key: float32 [2048, 1024], P(('shard', 'replica'))
- grad_w_value: float32 [2048, 1024], P(('shard', 'replica'))
- grad_w_out: float32 [1024, 2048], P(('shard', 'replica'))
- grad_w_gate: float32 [2048, 4096], P(('shard', 'replica'))
- grad_w_up: float32 [2048, 4096], P(('shard', 'replica'))
- grad_w_down: float32 [4096, 2048], P(('shard', 'replica'))
- grad_gain_query: float32 [1024], P(('shard', 'replica'))
- grad_gain_key: float32 [1024], P(('shard', 'replica'))
- grad_gain_attn: float32 [2048], P(('shard', 'replica'))
- grad_gain_mlp: float32 [2048], P(('shard', 'replica'))
All inputs are finite; a program needn't handle non-finite values.
Results may differ from a plain program's by a relative error of at most 0.018.
Values may be sent and summed in bfloat16 or wider, within the bound.
A program may use at most 512 MiB of HBM per device.

v0:
```python
import math
import jax
import jax.numpy as jnp
from jax import lax
from jax.sharding import PartitionSpec as P

HD = 128
eps_norm = 1e-06
rope_theta = 500000.0


def rope_tables(length, half):
    position = jnp.arange(length).astype(jnp.float32)[:, None]
    exponent = jnp.arange(half).astype(jnp.float32) * (1.0 / half)
    angle = position * rope_theta ** (-exponent)
    return (jnp.cos(angle), jnp.sin(angle))


def rotate(field, wave_cos, wave_sin):
    half = field.shape[-1] // 2
    first_half = field[..., :half]
    second_half = field[..., half:]
    cos_part = wave_cos[None, :, None, :]
    sin_part = wave_sin[None, :, None, :]
    return jnp.concatenate(
        [
            first_half * cos_part - second_half * sin_part,
            second_half * cos_part + first_half * sin_part,
        ],
        axis=-1,
    )


def unrotate(field, wave_cos, wave_sin):
    half = field.shape[-1] // 2
    first_half = field[..., :half]
    second_half = field[..., half:]
    cos_part = wave_cos[None, :, None, :]
    sin_part = wave_sin[None, :, None, :]
    return jnp.concatenate(
        [
            first_half * cos_part + second_half * sin_part,
            second_half * cos_part - first_half * sin_part,
        ],
        axis=-1,
    )


def rms_scale(field):
    return lax.rsqrt(jnp.mean(field * field, axis=-1, keepdims=True) + eps_norm)


def norm_back(grad_out, field, scale, gain):
    weighted = grad_out * gain
    inner = jnp.mean(weighted * field, axis=-1, keepdims=True)
    grad_field = scale * weighted - field * scale**3 * inner
    grad_gain = jnp.sum(grad_out * field * scale, axis=0)
    return (grad_field, grad_gain)


def matmul(left, right):
    return jnp.dot(left, right, preferred_element_type=jnp.float32)


def attn_scores(query_rot, key_rot, causal):
    scores = jnp.einsum(
        "sqhd,skhd->shqk", query_rot, key_rot, preferred_element_type=jnp.float32
    ) / math.sqrt(HD)
    return jnp.where(causal, scores, -jnp.inf)


def body(
    x_in,
    cotangent,
    w_query,
    w_key,
    w_value,
    w_out,
    w_gate,
    w_up,
    w_down,
    gain_query,
    gain_key,
    gain_attn,
    gain_mlp,
):
    attn_set = (
        lax.all_gather(w_query, "shard", axis=0, tiled=True),
        lax.all_gather(w_key, "shard", axis=0, tiled=True),
        lax.all_gather(w_value, "shard", axis=0, tiled=True),
        lax.all_gather(w_out, "shard", axis=0, tiled=True),
        lax.all_gather(gain_query, "shard", axis=0, tiled=True),
        lax.all_gather(gain_key, "shard", axis=0, tiled=True),
        lax.all_gather(gain_attn, "shard", axis=0, tiled=True),
    )
    mlp_set = (
        lax.all_gather(w_gate, "shard", axis=0, tiled=True),
        lax.all_gather(w_up, "shard", axis=0, tiled=True),
        lax.all_gather(w_down, "shard", axis=0, tiled=True),
        lax.all_gather(gain_mlp, "shard", axis=0, tiled=True),
    )
    seq_count, length, model_width = x_in.shape
    att_width = attn_set[0].shape[1]
    head_count = att_width // HD
    four_shape = (seq_count, length, head_count, HD)
    token_rows = x_in.reshape(seq_count * length, model_width)
    wave_cos, wave_sin = rope_tables(length, HD // 2)
    causal = jnp.arange(length)[:, None] >= jnp.arange(length)[None, :]
    query_proj = matmul(token_rows, attn_set[0])
    query_scale = rms_scale(query_proj)
    query_normed = query_proj * query_scale * attn_set[4].astype(jnp.float32)
    key_proj = matmul(token_rows, attn_set[1])
    key_scale = rms_scale(key_proj)
    key_normed = key_proj * key_scale * attn_set[5].astype(jnp.float32)
    value_four = matmul(token_rows, attn_set[2]).astype(jnp.bfloat16).reshape(four_shape)
    query_rot = rotate(query_normed.reshape(four_shape), wave_cos, wave_sin).astype(jnp.bfloat16)
    key_rot = rotate(key_normed.reshape(four_shape), wave_cos, wave_sin).astype(jnp.bfloat16)
    scores = attn_scores(query_rot, key_rot, causal)
    row_peak = jnp.max(scores, axis=-1, keepdims=True)
    log_total = row_peak + jnp.log(jnp.sum(jnp.exp(scores - row_peak), axis=-1, keepdims=True))
    probs_low = jnp.exp(scores - log_total).astype(jnp.bfloat16)
    attn_mixed = jnp.einsum(
        "shqk,skhd->sqhd", probs_low, value_four, preferred_element_type=jnp.float32
    )
    attn_mixed = attn_mixed.astype(jnp.bfloat16).reshape(-1, att_width)
    attn_proj = matmul(attn_mixed, attn_set[3])
    attn_scale = rms_scale(attn_proj)
    residual = token_rows.astype(jnp.float32) + attn_proj * attn_scale * attn_set[6].astype(
        jnp.float32
    )
    residual_low = residual.astype(jnp.bfloat16)
    gate_proj = matmul(residual_low, mlp_set[0])
    up_proj = matmul(residual_low, mlp_set[1])
    gate_sigmoid = jax.nn.sigmoid(gate_proj)
    gate_silu = gate_proj * gate_sigmoid
    hidden = (gate_silu * up_proj).astype(jnp.bfloat16)
    down_proj = matmul(hidden, mlp_set[2])
    down_scale = rms_scale(down_proj)
    output = residual + down_proj * down_scale * mlp_set[3].astype(jnp.float32)
    mlp_back = (
        lax.all_gather(w_gate, "shard", axis=0, tiled=True),
        lax.all_gather(w_up, "shard", axis=0, tiled=True),
        lax.all_gather(w_down, "shard", axis=0, tiled=True),
        lax.all_gather(gain_mlp, "shard", axis=0, tiled=True),
    )
    grad_output = cotangent.reshape(-1, model_width).astype(jnp.float32)
    grad_down, grad_gain_mlp = norm_back(
        grad_output, down_proj, down_scale, mlp_back[3].astype(jnp.float32)
    )
    grad_down = grad_down.astype(jnp.bfloat16)
    grad_w_down = matmul(hidden.T, grad_down)
    grad_hidden = matmul(grad_down, mlp_back[2].T)
    grad_gate = (
        grad_hidden * up_proj * gate_sigmoid * (1.0 + gate_proj * (1.0 - gate_sigmoid))
    ).astype(jnp.bfloat16)
    grad_up = (grad_hidden * gate_silu).astype(jnp.bfloat16)
    grad_w_gate = matmul(residual_low.T, grad_gate)
    grad_w_up = matmul(residual_low.T, grad_up)
    grad_residual = grad_output + matmul(grad_gate, mlp_back[0].T) + matmul(grad_up, mlp_back[1].T)
    mlp_grads = (grad_w_gate, grad_w_up, grad_w_down, grad_gain_mlp)
    mlp_half = (
        lax.psum_scatter(
            mlp_grads[0].astype(jnp.bfloat16), "shard", scatter_dimension=0, tiled=True
        ).astype(jnp.float32),
        lax.psum_scatter(
            mlp_grads[1].astype(jnp.bfloat16), "shard", scatter_dimension=0, tiled=True
        ).astype(jnp.float32),
        lax.psum_scatter(
            mlp_grads[2].astype(jnp.bfloat16), "shard", scatter_dimension=0, tiled=True
        ).astype(jnp.float32),
        lax.psum_scatter(
            mlp_grads[3].astype(jnp.bfloat16), "shard", scatter_dimension=0, tiled=True
        ).astype(jnp.float32),
    )
    mlp_owned = (
        lax.psum_scatter(mlp_half[0], "replica", scatter_dimension=0, tiled=True),
        lax.psum_scatter(mlp_half[1], "replica", scatter_dimension=0, tiled=True),
        lax.psum_scatter(mlp_half[2], "replica", scatter_dimension=0, tiled=True),
        lax.psum_scatter(mlp_half[3], "replica", scatter_dimension=0, tiled=True),
    )
    attn_back = (
        lax.all_gather(w_query, "shard", axis=0, tiled=True),
        lax.all_gather(w_key, "shard", axis=0, tiled=True),
        lax.all_gather(w_value, "shard", axis=0, tiled=True),
        lax.all_gather(w_out, "shard", axis=0, tiled=True),
        lax.all_gather(gain_query, "shard", axis=0, tiled=True),
        lax.all_gather(gain_key, "shard", axis=0, tiled=True),
        lax.all_gather(gain_attn, "shard", axis=0, tiled=True),
    )
    grad_attn, grad_gain_attn = norm_back(
        grad_residual, attn_proj, attn_scale, attn_back[6].astype(jnp.float32)
    )
    grad_attn = grad_attn.astype(jnp.bfloat16)
    grad_w_out = matmul(attn_mixed.T, grad_attn)
    grad_mixed = matmul(grad_attn, attn_back[3].T).astype(jnp.bfloat16).reshape(four_shape)
    probs_again = jnp.exp(attn_scores(query_rot, key_rot, causal) - log_total)
    grad_value = jnp.einsum(
        "shqk,sqhd->skhd",
        probs_again.astype(jnp.bfloat16),
        grad_mixed,
        preferred_element_type=jnp.float32,
    ).astype(jnp.bfloat16)
    grad_probs = jnp.einsum(
        "sqhd,skhd->shqk", grad_mixed, value_four, preferred_element_type=jnp.float32
    )
    grad_scores = probs_again * (
        grad_probs - jnp.sum(probs_again * grad_probs, axis=-1, keepdims=True)
    )
    grad_scores = (grad_scores / math.sqrt(HD)).astype(jnp.bfloat16)
    grad_qrot = jnp.einsum(
        "shqk,skhd->sqhd", grad_scores, key_rot, preferred_element_type=jnp.float32
    )
    grad_krot = jnp.einsum(
        "shqk,sqhd->skhd", grad_scores, query_rot, preferred_element_type=jnp.float32
    )
    grad_qnormed = unrotate(grad_qrot, wave_cos, wave_sin).reshape(-1, att_width)
    grad_knormed = unrotate(grad_krot, wave_cos, wave_sin).reshape(-1, att_width)
    grad_query, grad_gain_query = norm_back(
        grad_qnormed, query_proj, query_scale, attn_back[4].astype(jnp.float32)
    )
    grad_key, grad_gain_key = norm_back(
        grad_knormed, key_proj, key_scale, attn_back[5].astype(jnp.float32)
    )
    grad_query = grad_query.astype(jnp.bfloat16)
    grad_key = grad_key.astype(jnp.bfloat16)
    grad_value = grad_value.reshape(-1, att_width)
    grad_w_query = matmul(token_rows.T, grad_query)
    grad_w_key = matmul(token_rows.T, grad_key)
    grad_w_value = matmul(token_rows.T, grad_value)
    grad_input = (
        grad_residual
        + matmul(grad_query, attn_back[0].T)
        + matmul(grad_key, attn_back[1].T)
        + matmul(grad_value, attn_back[2].T)
    )
    attn_grads = (
        grad_w_query,
        grad_w_key,
        grad_w_value,
        grad_w_out,
        grad_gain_query,
        grad_gain_key,
        grad_gain_attn,
    )
    attn_half = (
        lax.psum_scatter(
            attn_grads[0].astype(jnp.bfloat16), "shard", scatter_dimension=0, tiled=True
        ).astype(jnp.float32),
        lax.psum_scatter(
            attn_grads[1].astype(jnp.bfloat16), "shard", scatter_dimension=0, tiled=True
        ).astype(jnp.float32),
        lax.psum_scatter(
            attn_grads[2].astype(jnp.bfloat16), "shard", scatter_dimension=0, tiled=True
        ).astype(jnp.float32),
        lax.psum_scatter(
            attn_grads[3].astype(jnp.bfloat16), "shard", scatter_dimension=0, tiled=True
        ).astype(jnp.float32),
        lax.psum_scatter(
            attn_grads[4].astype(jnp.bfloat16), "shard", scatter_dimension=0, tiled=True
        ).astype(jnp.float32),
        lax.psum_scatter(
            attn_grads[5].astype(jnp.bfloat16), "shard", scatter_dimension=0, tiled=True
        ).astype(jnp.float32),
        lax.psum_scatter(
            attn_grads[6].astype(jnp.bfloat16), "shard", scatter_dimension=0, tiled=True
        ).astype(jnp.float32),
    )
    attn_owned = (
        lax.psum_scatter(attn_half[0], "replica", scatter_dimension=0, tiled=True),
        lax.psum_scatter(attn_half[1], "replica", scatter_dimension=0, tiled=True),
        lax.psum_scatter(attn_half[2], "replica", scatter_dimension=0, tiled=True),
        lax.psum_scatter(attn_half[3], "replica", scatter_dimension=0, tiled=True),
        lax.psum_scatter(attn_half[4], "replica", scatter_dimension=0, tiled=True),
        lax.psum_scatter(attn_half[5], "replica", scatter_dimension=0, tiled=True),
        lax.psum_scatter(attn_half[6], "replica", scatter_dimension=0, tiled=True),
    )
    return (
        output.astype(jnp.bfloat16).reshape(x_in.shape),
        grad_input.reshape(x_in.shape),
        attn_owned[0],
        attn_owned[1],
        attn_owned[2],
        attn_owned[3],
        mlp_owned[0],
        mlp_owned[1],
        mlp_owned[2],
        attn_owned[4],
        attn_owned[5],
        attn_owned[6],
        mlp_owned[3],
    )


def solution(mesh):
    return jax.shard_map(
        body,
        mesh=mesh,
        in_specs=(
            P(("shard", "replica"), None, None),
            P(("shard", "replica"), None, None),
            P("shard", None),
            P("shard", None),
            P("shard", None),
            P("shard", None),
            P("shard", None),
            P("shard", None),
            P("shard", None),
            P("shard"),
            P("shard"),
            P("shard"),
            P("shard"),
        ),
        out_specs=(
            P(("shard", "replica"), None, None),
            P(("shard", "replica"), None, None),
            P(("shard", "replica"), None),
            P(("shard", "replica"), None),
            P(("shard", "replica"), None),
            P(("shard", "replica"), None),
            P(("shard", "replica"), None),
            P(("shard", "replica"), None),
            P(("shard", "replica"), None),
            P(("shard", "replica")),
            P(("shard", "replica")),
            P(("shard", "replica")),
            P(("shard", "replica")),
        ),
        check_vma=False,
    )
```

profile of v0, /device:TPU:0, one launch (start us, length us, event | category | flops | bytes accessed | tf_op | source)
XLA Modules:
  0.0 2560.4 jit_solution(11630051221962567769)
XLA Ops:
  31.1 37.9 %all-gather.14.cloned.1.call-done = bf16[2048,1024]{1,0:T(8,128)(2,1)} async-done(((bf16[1024,1024]{1,0:T(8,128)(2,1)}), bf16[2048,1024]{1,0:T(8,128)(2,1)}) %all-gather.14.cloned.1.call-update) | async-done | bytes 4194320 | tf_op jit(solution)/shard_map/all_gather | solution.py:89
  73.1 54.3 %all-gather.12.cloned.1.call-done = bf16[2048,1024]{1,0:T(8,128)(2,1)} async-done(((bf16[1024,1024]{1,0:T(8,128)(2,1)}), bf16[2048,1024]{1,0:T(8,128)(2,1)}) %all-gather.12.cloned.1.call-update) | async-done | bytes 4194320 | tf_op jit(solution)/shard_map/all_gather | solution.py:88
  133.5 52.2 %all-gather.10.cloned.1.call-done = bf16[2048,1024]{1,0:T(8,128)(2,1)} async-done(((bf16[1024,1024]{1,0:T(8,128)(2,1)}), bf16[2048,1024]{1,0:T(8,128)(2,1)}) %all-gather.10.cloned.1.call-update) | async-done | bytes 4194320 | tf_op jit(solution)/shard_map/all_gather | solution.py:90
  188.9 54.9 %all-gather.16.cloned.1.call-done = bf16[1024,2048]{1,0:T(8,128)(2,1)} async-done(((bf16[512,2048]{1,0:T(8,128)(2,1)}), bf16[1024,2048]{1,0:T(8,128)(2,1)}) %all-gather.16.cloned.1.call-update) | async-done | bytes 4194320 | tf_op jit(solution)/shard_map/all_gather | solution.py:91
  247.1 197.0 %all-gather.18.cloned.1.call-done = bf16[2048,4096]{1,0:T(8,128)(2,1)} async-done(((bf16[1024,4096]{1,0:T(8,128)(2,1)}), bf16[2048,4096]{1,0:T(8,128)(2,1)}) %all-gather.18.cloned.1.call-update) | async-done | bytes 16777232 | tf_op jit(solution)/shard_map/all_gather | solution.py:97
  444.1 9.4 fusion.64
  453.5 190.8 %all-gather.20.cloned.1.call-done = bf16[2048,4096]{1,0:T(8,128)(2,1)} async-done(((bf16[1024,4096]{1,0:T(8,128)(2,1)}), bf16[2048,4096]{1,0:T(8,128)(2,1)}) %all-gather.20.cloned.1.call-update) | async-done | bytes 16777232 | tf_op jit(solution)/shard_map/all_gather | solution.py:98
  644.4 11.3 multiply_convert_fusion.2
  655.6 189.2 %all-gather.22.cloned.1.call-done = bf16[4096,2048]{1,0:T(8,128)(2,1)} async-done(((bf16[2048,2048]{1,0:T(8,128)(2,1)}), bf16[4096,2048]{1,0:T(8,128)(2,1)}) %all-gather.22.cloned.1.call-update) | async-done | bytes 16777232 | tf_op jit(solution)/shard_map/all_gather | solution.py:99
  844.8 8.9 multiply_reduce_fusion.2
  854.7 14.4 multiply_convert_fusion
  869.1 12.7 convolution_add_fusion.4
  881.8 13.7 multiply_reduce_fusion
  930.7 8.5 convolution_convert_fusion
  940.5 8.1 convolution_convert_fusion.2
  949.8 8.1 convolution_convert_fusion.1
  963.8 52.5 %reduce-scatter.23.cloned.1.call-done = bf16[1024,1024]{0,1:T(8,128)(2,1)} async-done(((bf16[2048,1024]{0,1:T(8,128)(2,1)}), bf16[1024,1024]{0,1:T(8,128)(2,1)}) %reduce-scatter.23.cloned.1.call-update) | async-done | bytes 2097168 | tf_op jit(solution)/shard_map/reduce_scatter | solution.py:249
  1020.5 52.3 %reduce-scatter.27.cloned.1.call-done = bf16[512,2048]{1,0:T(8,128)(2,1)} async-done(((bf16[1024,2048]{1,0:T(8,128)(2,1)}), bf16[512,2048]{1,0:T(8,128)(2,1)}) %reduce-scatter.27.cloned.1.call-update) | async-done | bytes 2097168 | tf_op jit(solution)/shard_map/reduce_scatter | solution.py:255
  1077.0 52.5 %reduce-scatter.21.cloned.1.call-done = bf16[1024,1024]{0,1:T(8,128)(2,1)} async-done(((bf16[2048,1024]{0,1:T(8,128)(2,1)}), bf16[1024,1024]{0,1:T(8,128)(2,1)}) %reduce-scatter.21.cloned.1.call-update) | async-done | bytes 2097168 | tf_op jit(solution)/shard_map/reduce_scatter | solution.py:246
  1133.7 187.2 %reduce-scatter.39.cloned.1.call-done = bf16[2048,2048]{1,0:T(8,128)(2,1)} async-done(((bf16[4096,2048]{1,0:T(8,128)(2,1)}), bf16[2048,2048]{1,0:T(8,128)(2,1)}) %reduce-scatter.39.cloned.1.call-update) | async-done | bytes 8388624 | tf_op jit(solution)/shard_map/reduce_scatter | solution.py:168
  1320.9 11.8 convert_element_type.288
  1332.7 179.7 %reduce-scatter.31.cloned.1.call-done = bf16[1024,4096]{1,0:T(8,128)(2,1)} async-done(((bf16[2048,4096]{1,0:T(8,128)(2,1)}), bf16[1024,4096]{1,0:T(8,128)(2,1)}) %reduce-scatter.31.cloned.1.call-update) | async-done | bytes 8388624 | tf_op jit(solution)/shard_map/reduce_scatter | solution.py:162
  1512.4 11.9 convert_element_type.284
  1524.6 179.2 %reduce-scatter.35.cloned.1.call-done = bf16[1024,4096]{1,0:T(8,128)(2,1)} async-done(((bf16[2048,4096]{1,0:T(8,128)(2,1)}), bf16[1024,4096]{1,0:T(8,128)(2,1)}) %reduce-scatter.35.cloned.1.call-update) | async-done | bytes 8388624 | tf_op jit(solution)/shard_map/reduce_scatter | solution.py:165
  1703.8 11.6 convert_element_type.286
  1726.8 59.8 %all-reduce.8 = (f32[512]{0:T(512)S(1)}, f32[512]{0:T(512)S(1)}, f32[1024]{0:T(1024)S(1)}, f32[1024]{0:T(1024)S(1)}) all-reduce(f32[512]{0:T(512)S(1)} %dynamic-slice_convert_fusion.3, f32[512]{0:T(512)S(1)} %dynamic-slice_convert_fusion.2, ...), channel_id=17, replica_groups=mesh['shard'=2,'replica'=16] {'replica'}, use_global_device_ids=true, to_apply=%region_27.28.clone | all-reduce | flops 3072 | bytes 24576
  1797.7 59.8 %reduce-scatter.45.cloned.1.call-done = f32[64,1024]{1,0:T(8,128)} async-done(((f32[1024,1024]{1,0:T(8,128)}), f32[64,1024]{1,0:T(8,128)}) %reduce-scatter.45.cloned.1.call-update) | async-done | bytes 262160
  1857.6 76.2 %reduce-scatter.29.cloned.1.call-done = f32[32,2048]{1,0:T(8,128)} async-done(((f32[512,2048]{1,0:T(8,128)}), f32[32,2048]{1,0:T(8,128)}) %reduce-scatter.29.cloned.1.call-update) | async-done | bytes 262160 | tf_op jit(solution)/shard_map/reduce_scatter | solution.py:272
  1933.7 76.1 %reduce-scatter.43.cloned.1.call-done = f32[64,1024]{1,0:T(8,128)} async-done(((f32[1024,1024]{1,0:T(8,128)}), f32[64,1024]{1,0:T(8,128)}) %reduce-scatter.43.cloned.1.call-update) | async-done | bytes 262160
  2009.9 181.1 %reduce-scatter.41.cloned.1.call-done = f32[128,2048]{1,0:T(8,128)} async-done(((f32[2048,2048]{1,0:T(8,128)}), f32[128,2048]{1,0:T(8,128)}) %reduce-scatter.41.cloned.1.call-update) | async-done | bytes 1048592 | tf_op jit(solution)/shard_map/reduce_scatter | solution.py:178
  2191.0 181.0 %reduce-scatter.33.cloned.1.call-done = f32[64,4096]{1,0:T(8,128)} async-done(((f32[1024,4096]{1,0:T(8,128)}), f32[64,4096]{1,0:T(8,128)}) %reduce-scatter.33.cloned.1.call-update) | async-done | bytes 1048592 | tf_op jit(solution)/shard_map/reduce_scatter | solution.py:176
  2372.0 181.1 %reduce-scatter.37.cloned.1.call-done = f32[64,4096]{1,0:T(8,128)} async-done(((f32[1024,4096]{1,0:T(8,128)}), f32[64,4096]{1,0:T(8,128)}) %reduce-scatter.37.cloned.1.call-update) | async-done | bytes 1048592 | tf_op jit(solution)/shard_map/reduce_scatter | solution.py:177
  (224 shorter events, 117.0 us)
Async XLA Ops:
  7.2 61.9 %all-gather.14.cloned.1.call-start = ((), (), s32[]{:S(2)}) async-start(), calls=%async_computation.16 | async-start | bytes 6291456 | tf_op jit(solution)/shard_map/all_gather | solution.py:89
  7.9 119.5 %all-gather.12.cloned.1.call-start = ((), (), s32[]{:S(2)}) async-start(), calls=%async_computation.15 | async-start | bytes 6291456 | tf_op jit(solution)/shard_map/all_gather | solution.py:88
  8.7 177.0 %all-gather.10.cloned.1.call-start = ((), (), s32[]{:S(2)}) async-start(), calls=%async_computation.14 | async-start | bytes 6291456 | tf_op jit(solution)/shard_map/all_gather | solution.py:90
  9.4 234.5 %all-gather.16.cloned.1.call-start = ((), (), s32[]{:S(2)}) async-start(), calls=%async_computation.17 | async-start | bytes 6291456 | tf_op jit(solution)/shard_map/all_gather | solution.py:91
  10.0 434.1 %all-gather.18.cloned.1.call-start = ((), (), s32[]{:S(2)}) async-start(), calls=%async_computation.18 | async-start | bytes 25165824 | tf_op jit(solution)/shard_map/all_gather | solution.py:97
  10.6 633.8 %all-gather.20.cloned.1.call-start = ((), (), s32[]{:S(2)}) async-start(), calls=%async_computation.19 | async-start | bytes 25165824 | tf_op jit(solution)/shard_map/all_gather | solution.py:98
  11.2 57.9 %copy-start = (bf16[1,128,2048]{2,1,0:T(8,128)(2,1)S(1)}, bf16[1,128,2048]{2,1,0:T(8,128)(2,1)}, u32[]{:S(2)}) copy-start(bf16[1,128,2048]{2,1,0:T(8,128)(2,1)} %param.13) | copy-start | bytes 1572868
  11.2 833.6 %all-gather.22.cloned.1.call-start = ((), (), s32[]{:S(2)}) async-start(), calls=%async_computation.20 | async-start | bytes 25165824 | tf_op jit(solution)/shard_map/all_gather | solution.py:99
  11.9 947.6 %reduce-scatter.25.cloned.1.call-start = ((), (), s32[]{:S(2)}) async-start(), calls=%async_computation.23 | async-start | bytes 6291456 | tf_op jit(solution)/shard_map/reduce_scatter | solution.py:252
  72.6 57.7 %copy-start.36 = (f32[128]{0:T(128)}, f32[128]{0:T(128)S(1)}, u32[]{:S(2)}) copy-start(f32[128]{0:T(128)S(1)} %get-tuple-element.78) | copy-start | bytes 1540
  133.4 110.5 %copy-start.5 = (f32[8,128,128]{1,2,0:T(8,128)}, f32[8,128,128]{1,2,0:T(8,128)S(1)}, u32[]{:S(2)}) copy-start(f32[8,128,128]{1,2,0:T(8,128)S(1)} %get-tuple-element.90) | copy-start | bytes 1572868
  133.5 113.4 %copy-start.31 = (f32[8,128]{1,0:T(8,128)}, f32[8,128]{1,0:T(8,128)S(1)}, u32[]{:S(2)}) copy-start(f32[8,128]{1,0:T(8,128)S(1)} %log_add_fusion) | copy-start | bytes 12292
  188.6 55.2 %copy-start.24 = (bf16[16,8,8,128]{3,2,1,0:T(8,128)(2,1)}, bf16[16,8,8,128]{3,2,1,0:T(8,128)(2,1)S(1)}, u32[]{:S(2)}) copy-start(bf16[16,8,8,128]{3,2,1,0:T(8,128)(2,1)S(1)} %fusion.10) | copy-start | bytes 786436
  188.9 264.6 %copy-start.22 = (bf16[8,128,128]{2,1,0:T(8,128)(2,1)}, bf16[8,128,128]{2,1,0:T(8,128)(2,1)S(1)}, u32[]{:S(2)}) copy-start(bf16[8,128,128]{2,1,0:T(8,128)(2,1)S(1)} %convolution_convert_fusion.5) | copy-start | bytes 786436
  853.8 15.3 copy-start.46
  853.8 41.8 %copy-start.38 = (f32[128]{0:T(128)}, f32[128]{0:T(128)S(1)}, u32[]{:S(2)}) copy-start(f32[128]{0:T(128)S(1)} %get-tuple-element.84) | copy-start | bytes 1540
  905.0 111.2 %reduce-scatter.23.cloned.1.call-start = ((), (), s32[]{:S(2)}) async-start(), calls=%async_computation.22 | async-start | bytes 6291456 | tf_op jit(solution)/shard_map/reduce_scatter | solution.py:249
  919.4 153.4 %reduce-scatter.27.cloned.1.call-start = ((), (), s32[]{:S(2)}) async-start(), calls=%async_computation.24 | async-start | bytes 6291456 | tf_op jit(solution)/shard_map/reduce_scatter | solution.py:255
  922.8 206.8 %reduce-scatter.21.cloned.1.call-start = ((), (), s32[]{:S(2)}) async-start(), calls=%async_computation.21 | async-start | bytes 6291456 | tf_op jit(solution)/shard_map/reduce_scatter | solution.py:246
  929.7 391.2 %reduce-scatter.39.cloned.1.call-start = ((), (), s32[]{:S(2)}) async-start(), calls=%async_computation.30 | async-start | bytes 25165824 | tf_op jit(solution)/shard_map/reduce_scatter | solution.py:168
  939.3 573.1 %reduce-scatter.31.cloned.1.call-start = ((), (), s32[]{:S(2)}) async-start(), calls=%async_computation.26 | async-start | bytes 25165824 | tf_op jit(solution)/shard_map/reduce_scatter | solution.py:162
  948.6 755.1 %reduce-scatter.35.cloned.1.call-start = ((), (), s32[]{:S(2)}) async-start(), calls=%async_computation.28 | async-start | bytes 25165824 | tf_op jit(solution)/shard_map/reduce_scatter | solution.py:165
  958.0 839.8 %reduce-scatter.47.cloned.1.call-start = ((), (), s32[]{:S(2)}) async-start(), calls=%async_computation.34 | async-start | bytes 4456448
  963.7 893.8 %reduce-scatter.45.cloned.1.call-start = ((), (), s32[]{:S(2)}) async-start(), calls=%async_computation.33 | async-start | bytes 4456448
  1020.4 913.3 %reduce-scatter.29.cloned.1.call-start = ((), (), s32[]{:S(2)}) async-start(), calls=%async_computation.25 | async-start | bytes 4456448 | tf_op jit(solution)/shard_map/reduce_scatter | solution.py:272
  1076.9 932.9 %reduce-scatter.43.cloned.1.call-start = ((), (), s32[]{:S(2)}) async-start(), calls=%async_computation.32 | async-start | bytes 4456448
  1133.7 1057.3 %reduce-scatter.41.cloned.1.call-start = ((), (), s32[]{:S(2)}) async-start(), calls=%async_computation.31 | async-start | bytes 17825792 | tf_op jit(solution)/shard_map/reduce_scatter | solution.py:178
  1332.7 1039.3 %reduce-scatter.33.cloned.1.call-start = ((), (), s32[]{:S(2)}) async-start(), calls=%async_computation.27 | async-start | bytes 17825792 | tf_op jit(solution)/shard_map/reduce_scatter | solution.py:176
  1524.3 1028.8 %reduce-scatter.37.cloned.1.call-start = ((), (), s32[]{:S(2)}) async-start(), calls=%async_computation.29 | async-start | bytes 17825792 | tf_op jit(solution)/shard_map/reduce_scatter | solution.py:177
  1715.4 73.5 %copy-start.4 = (f32[128,2048]{1,0:T(8,128)S(1)}, f32[128,2048]{1,0:T(8,128)}, u32[]{:S(2)}) copy-start(f32[128,2048]{1,0:T(8,128)} %get-tuple-element.97) | copy-start | bytes 3145732
  1715.4 73.5 %copy-start.21 = (bf16[128,1024]{1,0:T(8,128)(2,1)S(1)}, bf16[128,1024]{1,0:T(8,128)(2,1)}, u32[]{:S(2)}) copy-start(bf16[128,1024]{1,0:T(8,128)(2,1)} %copy-done.20) | copy-start | bytes 786436
  1715.4 77.3 %copy-start.19 = (bf16[128,1024]{1,0:T(8,128)(2,1)S(1)}, bf16[128,1024]{1,0:T(8,128)(2,1)}, u32[]{:S(2)}) copy-start(bf16[128,1024]{1,0:T(8,128)(2,1)} %copy-done.18) | copy-start | bytes 786436
  (41 other events, 142.2 us)
Sparse Core Ops, SparseCore 0:
  9.5 59.4 all-gather.13
  70.6 56.7 all-gather.11
  128.9 56.7 all-gather.9
  187.1 56.7 all-gather.15
  245.2 198.8 all-gather.17
  445.5 198.8 all-gather.19
  645.9 198.8 all-gather.21
  905.1 54.3 reduce-scatter.24
  961.8 54.3 reduce-scatter.22
  1018.4 54.3 reduce-scatter.26
  1075.1 54.3 reduce-scatter.20
  1131.7 189.2 reduce-scatter.38
  1323.2 189.1 reduce-scatter.30
  1514.6 189.1 reduce-scatter.34
  1708.1 73.2 reduce-scatter.46
  1785.7 71.8 reduce-scatter.44
  1861.8 71.8 reduce-scatter.28
  1938.0 71.8 reduce-scatter.42
  2014.5 176.4 reduce-scatter.40
  2195.5 176.4 reduce-scatter.32
  2376.7 176.4 reduce-scatter.36
where the time goes:
time: 2570 us; the launch traced here: 2560 us
  waiting for transfers between devices  2240 us (87%)
  matrix products  138 us (5%)
  blocking collectives  85.3 us (3%)
  other arithmetic  50.8 us (2%)
  local copies, waits for them, and re-layouts  26.2 us (1%)
    all_gather x1, waiting for transfers between devices, body(): lax.all_gather(w_gate, 'shard', axis=0, tiled=True)  197 us
    all_gather x1, waiting for transfers between devices, body(): lax.all_gather(w_up, 'shard', axis=0, tiled=True)  191 us
    all_gather x1, waiting for transfers between devices, body(): lax.all_gather(w_down, 'shard', axis=0, tiled=True)  189 us
    reduce_scatter x1, waiting for transfers between devices, body(): lax.psum_scatter(mlp_grads[2].astype(jnp.bfloat16), 'shard', scatter_dime...  187 us
    reduce_scatter x1, waiting for transfers between devices, body(): lax.psum_scatter(mlp_half[1], 'replica', scatter_dimension=0, tiled=True)  181 us
    reduce_scatter x1, waiting for transfers between devices, body(): lax.psum_scatter(mlp_half[2], 'replica', scatter_dimension=0, tiled=True)  181 us
    reduce_scatter x1, waiting for transfers between devices, body(): lax.psum_scatter(mlp_half[0], 'replica', scatter_dimension=0, tiled=True)  181 us
    reduce_scatter x1, waiting for transfers between devices, body(): lax.psum_scatter(mlp_grads[0].astype(jnp.bfloat16), 'shard', scatter_dime...  180 us
  transfers between devices with their start and end apart: 21, of which 20 were waited for; matrix products, arithmetic and copies ran while one was open for 6% of the time, Pallas kernels for 0%

commit v1 on v0

--- a/solution.py
+++ b/solution.py
@@ -7,6 +7,18 @@
 HD = 128
 eps_norm = 1e-06
 rope_theta = 500000.0
+
+
+def collect(x, axis, dim):
+    ways, here = (lax.axis_size(axis), lax.axis_index(axis))
+    grown, reach = (x, 1)
+    while reach < ways:
+        theirs = lax.ppermute(grown, axis, [(d, d ^ reach) for d in range(ways)])
+        mine_first = jnp.concatenate([grown, theirs], axis=dim)
+        theirs_first = jnp.concatenate([theirs, grown], axis=dim)
+        grown = jnp.where(here & reach == 0, mine_first, theirs_first)
+        reach = 2 * reach
+    return grown
 
 
 def rope_tables(length, half):
@@ -95,7 +107,7 @@
     )
     mlp_set = (
         lax.all_gather(w_gate, "shard", axis=0, tiled=True),
-        lax.all_gather(w_up, "shard", axis=0, tiled=True),
+        collect(w_up, "shard", 0),
         lax.all_gather(w_down, "shard", axis=0, tiled=True),
         lax.all_gather(gain_mlp, "shard", axis=0, tiled=True),
     )

time: 2570 us -> 2670 us (1.039)
  blocking collectives: 85.3 us -> 396 us
  waiting for transfers between devices: 2240 us -> 2010 us
    all_gather x1, blocking collectives: 5.29 us -> 316 us  [body(): lax.all_gather(gain_key, 'shard', axis=0, tiled=True)]
    all_gather x1, waiting for transfers between devices: 54.3 us -> 0.02 us  [body(): lax.all_gather(w_query, 'shard', axis=0, tiled=True)]
    all_gather x1, waiting for transfers between devices: 52.2 us -> 0.02 us  [body(): lax.all_gather(w_value, 'shard', axis=0, tiled=True)]
    all_gather x1, waiting for transfers between devices: 37.9 us -> 0.02 us  [body(): lax.all_gather(w_key, 'shard', axis=0, tiled=True)]
    all_gather x1, waiting for transfers between devices: 54.9 us -> 21 us  [body(): lax.all_gather(w_out, 'shard', axis=0, tiled=True)]
    all_gather x1, waiting for transfers between devices: 191 us -> 159 us  [body(): lax.all_gather(w_up, 'shard', axis=0, tiled=True)]
  transfers between devices with their start and end apart: 21 -> 22, of which waited for: 20 -> 17; matrix products, arithmetic and copies ran while one was open for 6% -> 7% of each run, Pallas kernels for 0% -> 0%
where the time goes in v1:
time: 2670 us; the launch traced here: 2660 us
  waiting for transfers between devices  2010 us (75%)
  blocking collectives  396 us (15%)
  matrix products  150 us (6%)
  other arithmetic  50.8 us (2%)
  local copies, waits for them, and re-layouts  27.3 us (1%)
    all_gather x1, blocking collectives, body(): lax.all_gather(gain_key, 'shard', axis=0, tiled=True)  316 us
    all_gather x1, waiting for transfers between devices, body(): lax.all_gather(w_gate, 'shard', axis=0, tiled=True)  197 us
    reduce_scatter x1, waiting for transfers between devices, body(): lax.psum_scatter(mlp_grads[2].astype(jnp.bfloat16), 'shard', scatter_dime...  187 us
    reduce_scatter x1, waiting for transfers between devices, body(): lax.psum_scatter(mlp_half[1], 'replica', scatter_dimension=0, tiled=True)  181 us
    reduce_scatter x1, waiting for transfers between devices, body(): lax.psum_scatter(mlp_half[2], 'replica', scatter_dimension=0, tiled=True)  181 us
    reduce_scatter x1, waiting for transfers between devices, body(): lax.psum_scatter(mlp_half[0], 'replica', scatter_dimension=0, tiled=True)  181 us
    reduce_scatter x1, waiting for transfers between devices, body(): lax.psum_scatter(mlp_grads[0].astype(jnp.bfloat16), 'shard', scatter_dime...  180 us
    reduce_scatter x1, waiting for transfers between devices, body(): lax.psum_scatter(mlp_grads[1].astype(jnp.bfloat16), 'shard', scatter_dime...  179 us
  transfers between devices with their start and end apart: 22, of which 17 were waited for; matrix products, arithmetic and copies ran while one was open for 7% of the time, Pallas kernels for 0%

profile of v1, /device:TPU:0, one launch (start us, length us, event | category | flops | bytes accessed | tf_op | source)
XLA Modules:
  0.0 2658.3 jit_solution(11696989344610504211)
XLA Ops:
  15.0 315.6 %all-gather.1 = bf16[2,1,512]{2,1,0:T(2,128)(2,1)S(1)} all-gather(bf16[1,1,512]{2,1,0:T(2,128)(2,1)S(1)} %reshape.315), channel_id=1, replica_groups=mesh['shard'=2,'replica'=16] {'shard'}, dimensions={0}, use_global_device_ids=true | all-gather | bytes 3072 | tf_op jit(solution)/shard_map/all_gather | solution.py:105
  335.1 4.5 all_gather.49
  358.0 21.0 all-gather.16.cloned.1.call-done
  382.3 197.0 %all-gather.18.cloned.1.call-done = bf16[2048,4096]{1,0:T(8,128)(2,1)} async-done(((bf16[1024,4096]{1,0:T(8,128)(2,1)}), bf16[2048,4096]{1,0:T(8,128)(2,1)}) %all-gather.18.cloned.1.call-update) | async-done | bytes 16777232 | tf_op jit(solution)/shard_map/all_gather | solution.py:109
  579.3 8.1 fusion.72
  588.8 20.2 multiply_convert_fusion.2
  609.0 170.6 %all-gather.20.cloned.1.call-done = bf16[4096,2048]{1,0:T(8,128)(2,1)} async-done(((bf16[2048,2048]{1,0:T(8,128)(2,1)}), bf16[4096,2048]{1,0:T(8,128)(2,1)}) %all-gather.20.cloned.1.call-update) | async-done | bytes 16777232 | tf_op jit(solution)/shard_map/all_gather | solution.py:111
  779.5 8.6 multiply_reduce_fusion.2
  789.1 18.7 multiply_convert_fusion
  807.8 13.4 convolution_add_fusion.4
  821.2 158.7 %all-gather.22.cloned.1.call-done = bf16[2048,4096]{1,0:T(8,128)(2,1)} async-done(((bf16[1024,4096]{1,0:T(8,128)(2,1)}), bf16[2048,4096]{1,0:T(8,128)(2,1)}) %all-gather.22.cloned.1.call-update) | async-done | bytes 16777232 | tf_op jit(solution)/shard_map/all_gather | solution.py:154
  980.0 13.7 multiply_reduce_fusion
  1029.0 8.5 convolution_convert_fusion
  1038.7 8.2 convolution_convert_fusion.2
  1048.1 8.1 convolution_convert_fusion.1
  1062.0 52.5 %reduce-scatter.23.cloned.1.call-done = bf16[1024,1024]{0,1:T(8,128)(2,1)} async-done(((bf16[2048,1024]{0,1:T(8,128)(2,1)}), bf16[1024,1024]{0,1:T(8,128)(2,1)}) %reduce-scatter.23.cloned.1.call-update) | async-done | bytes 2097168 | tf_op jit(solution)/shard_map/reduce_scatter | solution.py:261
  1118.7 52.3 %reduce-scatter.27.cloned.1.call-done = bf16[512,2048]{1,0:T(8,128)(2,1)} async-done(((bf16[1024,2048]{1,0:T(8,128)(2,1)}), bf16[512,2048]{1,0:T(8,128)(2,1)}) %reduce-scatter.27.cloned.1.call-update) | async-done | bytes 2097168 | tf_op jit(solution)/shard_map/reduce_scatter | solution.py:267
  1175.2 52.5 %reduce-scatter.21.cloned.1.call-done = bf16[1024,1024]{0,1:T(8,128)(2,1)} async-done(((bf16[2048,1024]{0,1:T(8,128)(2,1)}), bf16[1024,1024]{0,1:T(8,128)(2,1)}) %reduce-scatter.21.cloned.1.call-update) | async-done | bytes 2097168 | tf_op jit(solution)/shard_map/reduce_scatter | solution.py:258
  1231.9 187.2 %reduce-scatter.39.cloned.1.call-done = bf16[2048,2048]{1,0:T(8,128)(2,1)} async-done(((bf16[4096,2048]{1,0:T(8,128)(2,1)}), bf16[2048,2048]{1,0:T(8,128)(2,1)}) %reduce-scatter.39.cloned.1.call-update) | async-done | bytes 8388624 | tf_op jit(solution)/shard_map/reduce_scatter | solution.py:180
  1419.1 11.8 convert_element_type.288
  1431.1 179.5 %reduce-scatter.31.cloned.1.call-done = bf16[1024,4096]{1,0:T(8,128)(2,1)} async-done(((bf16[2048,4096]{1,0:T(8,128)(2,1)}), bf16[1024,4096]{1,0:T(8,128)(2,1)}) %reduce-scatter.31.cloned.1.call-update) | async-done | bytes 8388624 | tf_op jit(solution)/shard_map/reduce_scatter | solution.py:174
  1610.6 11.9 convert_element_type.284
  1622.6 179.4 %reduce-scatter.35.cloned.1.call-done = bf16[1024,4096]{1,0:T(8,128)(2,1)} async-done(((bf16[2048,4096]{1,0:T(8,128)(2,1)}), bf16[1024,4096]{1,0:T(8,128)(2,1)}) %reduce-scatter.35.cloned.1.call-update) | async-done | bytes 8388624 | tf_op jit(solution)/shard_map/reduce_scatter | solution.py:177
  1802.0 11.6 convert_element_type.286
  1818.0 6.7 all-reduce.9
  1824.9 59.8 %all-reduce.8 = (f32[512]{0:T(512)S(1)}, f32[512]{0:T(512)S(1)}, f32[1024]{0:T(1024)S(1)}, f32[1024]{0:T(1024)S(1)}) all-reduce(f32[512]{0:T(512)S(1)} %dynamic-slice_convert_fusion.3, f32[512]{0:T(512)S(1)} %dynamic-slice_convert_fusion.2, ...), channel_id=17, replica_groups=mesh['shard'=2,'replica'=16] {'replica'}, use_global_device_ids=true, to_apply=%region_27.28.clone | all-reduce | flops 3072 | bytes 24576
  1895.9 59.8 %reduce-scatter.45.cloned.1.call-done = f32[64,1024]{1,0:T(8,128)} async-done(((f32[1024,1024]{1,0:T(8,128)}), f32[64,1024]{1,0:T(8,128)}) %reduce-scatter.45.cloned.1.call-update) | async-done | bytes 262160
  1955.7 76.1 %reduce-scatter.29.cloned.1.call-done = f32[32,2048]{1,0:T(8,128)} async-done(((f32[512,2048]{1,0:T(8,128)}), f32[32,2048]{1,0:T(8,128)}) %reduce-scatter.29.cloned.1.call-update) | async-done | bytes 262160 | tf_op jit(solution)/shard_map/reduce_scatter | solution.py:284
  2031.8 76.1 %reduce-scatter.43.cloned.1.call-done = f32[64,1024]{1,0:T(8,128)} async-done(((f32[1024,1024]{1,0:T(8,128)}), f32[64,1024]{1,0:T(8,128)}) %reduce-scatter.43.cloned.1.call-update) | async-done | bytes 262160
  2107.9 181.2 %reduce-scatter.41.cloned.1.call-done = f32[128,2048]{1,0:T(8,128)} async-done(((f32[2048,2048]{1,0:T(8,128)}), f32[128,2048]{1,0:T(8,128)}) %reduce-scatter.41.cloned.1.call-update) | async-done | bytes 1048592 | tf_op jit(solution)/shard_map/reduce_scatter | solution.py:190
  2289.1 181.0 %reduce-scatter.33.cloned.1.call-done = f32[64,4096]{1,0:T(8,128)} async-done(((f32[1024,4096]{1,0:T(8,128)}), f32[64,4096]{1,0:T(8,128)}) %reduce-scatter.33.cloned.1.call-update) | async-done | bytes 1048592 | tf_op jit(solution)/shard_map/reduce_scatter | solution.py:188
  2470.1 181.2 %reduce-scatter.37.cloned.1.call-done = f32[64,4096]{1,0:T(8,128)} async-done(((f32[1024,4096]{1,0:T(8,128)}), f32[64,4096]{1,0:T(8,128)}) %reduce-scatter.37.cloned.1.call-update) | async-done | bytes 1048592 | tf_op jit(solution)/shard_map/reduce_scatter | solution.py:189
  (228 shorter events, 104.8 us)
Async XLA Ops:
  7.2 337.4 %all-gather.14.cloned.1.call-start = ((), (), s32[]{:S(2)}) async-start(), calls=%async_computation.16 | async-start | bytes 6291456 | tf_op jit(solution)/shard_map/all_gather | solution.py:101
  7.9 340.7 %all-gather.12.cloned.1.call-start = ((), (), s32[]{:S(2)}) async-start(), calls=%async_computation.15 | async-start | bytes 6291456 | tf_op jit(solution)/shard_map/all_gather | solution.py:100
  8.7 346.1 %all-gather.10.cloned.1.call-start = ((), (), s32[]{:S(2)}) async-start(), calls=%async_computation.14 | async-start | bytes 6291456 | tf_op jit(solution)/shard_map/all_gather | solution.py:102
  9.4 369.6 %all-gather.16.cloned.1.call-start = ((), (), s32[]{:S(2)}) async-start(), calls=%async_computation.17 | async-start | bytes 6291456 | tf_op jit(solution)/shard_map/all_gather | solution.py:103
  10.0 569.3 %all-gather.18.cloned.1.call-start = ((), (), s32[]{:S(2)}) async-start(), calls=%async_computation.18 | async-start | bytes 25165824 | tf_op jit(solution)/shard_map/all_gather | solution.py:109
  10.6 769.0 %all-gather.20.cloned.1.call-start = ((), (), s32[]{:S(2)}) async-start(), calls=%async_computation.19 | async-start | bytes 25165824 | tf_op jit(solution)/shard_map/all_gather | solution.py:111
  11.2 319.5 %copy-start.44 = (bf16[512]{0:T(512)(128)(2,1)S(1)}, bf16[512]{0:T(512)(128)(2,1)}, u32[]{:S(2)}) copy-start(bf16[512]{0:T(512)(128)(2,1)} %param.22) | copy-start | bytes 3076
  11.2 323.9 %copy-start.41 = (bf16[1024]{0:T(1024)(128)(2,1)S(1)}, bf16[1024]{0:T(1024)(128)(2,1)}, u32[]{:S(2)}) copy-start(bf16[1024]{0:T(1024)(128)(2,1)} %param.24) | copy-start | bytes 6148
  11.2 328.5 %copy-start.42 = (bf16[1024]{0:T(1024)(128)(2,1)S(1)}, bf16[1024]{0:T(1024)(128)(2,1)}, u32[]{:S(2)}) copy-start(bf16[1024]{0:T(1024)(128)(2,1)} %param.25) | copy-start | bytes 6148
  11.2 333.4 %copy-start = (bf16[1,128,2048]{2,1,0:T(8,128)(2,1)S(1)}, bf16[1,128,2048]{2,1,0:T(8,128)(2,1)}, u32[]{:S(2)}) copy-start(bf16[1,128,2048]{2,1,0:T(8,128)(2,1)} %param.13) | copy-start | bytes 1572868
  11.2 968.8 %all-gather.22.cloned.1.call-start = ((), (), s32[]{:S(2)}) async-start(), calls=%async_computation.20 | async-start | bytes 25165824 | tf_op jit(solution)/shard_map/all_gather | solution.py:154
  11.9 1045.8 %reduce-scatter.25.cloned.1.call-start = ((), (), s32[]{:S(2)}) async-start(), calls=%async_computation.23 | async-start | bytes 6291456 | tf_op jit(solution)/shard_map/reduce_scatter | solution.py:264
  12.0 575.4 %collective-permute-start = (bf16[1024,4096]{1,0:T(8,128)(2,1)}, bf16[1024,4096]{1,0:T(8,128)(2,1)}, u32[]{:S(2)}, u32[]{:S(2)}) collective-permute-start(bf16[1024,4096]{1,0:T(8,128)(2,1)} %param.20), channel_id=1, source_target_pairs={{0,16},{16,0},{1,17},{17,1},{2,18},{18,2},{3,19},{19,3},{4,20},{20... | collective-permute-start | bytes 25165832 | tf_op jit(solution)/shard_map/ppermute | solution.py:16
  354.7 27.3 %copy-start.32 = (f32[8,128]{1,0:T(8,128)}, f32[8,128]{1,0:T(8,128)S(1)}, u32[]{:S(2)}) copy-start(f32[8,128]{1,0:T(8,128)S(1)} %log_add_fusion) | copy-start | bytes 12292
  358.0 229.4 %copy-start.22 = (bf16[8,128,128]{2,1,0:T(8,128)(2,1)}, bf16[8,128,128]{2,1,0:T(8,128)(2,1)S(1)}, u32[]{:S(2)}) copy-start(bf16[8,128,128]{2,1,0:T(8,128)(2,1)S(1)} %convolution_convert_fusion.5) | copy-start | bytes 786436
  788.1 205.6 %copy-start.39 = (f32[128]{0:T(128)}, f32[128]{0:T(128)S(1)}, u32[]{:S(2)}) copy-start(f32[128]{0:T(128)S(1)} %get-tuple-element.84) | copy-start | bytes 1540
  1003.2 111.2 %reduce-scatter.23.cloned.1.call-start = ((), (), s32[]{:S(2)}) async-start(), calls=%async_computation.22 | async-start | bytes 6291456 | tf_op jit(solution)/shard_map/reduce_scatter | solution.py:261
  1017.6 153.4 %reduce-scatter.27.cloned.1.call-start = ((), (), s32[]{:S(2)}) async-start(), calls=%async_computation.24 | async-start | bytes 6291456 | tf_op jit(solution)/shard_map/reduce_scatter | solution.py:267
  1021.0 206.7 %reduce-scatter.21.cloned.1.call-start = ((), (), s32[]{:S(2)}) async-start(), calls=%async_computation.21 | async-start | bytes 6291456 | tf_op jit(solution)/shard_map/reduce_scatter | solution.py:258
  1028.0 391.1 %reduce-scatter.39.cloned.1.call-start = ((), (), s32[]{:S(2)}) async-start(), calls=%async_computation.30 | async-start | bytes 25165824 | tf_op jit(solution)/shard_map/reduce_scatter | solution.py:180
  1037.5 573.1 %reduce-scatter.31.cloned.1.call-start = ((), (), s32[]{:S(2)}) async-start(), calls=%async_computation.26 | async-start | bytes 25165824 | tf_op jit(solution)/shard_map/reduce_scatter | solution.py:174
  1046.9 755.1 %reduce-scatter.35.cloned.1.call-start = ((), (), s32[]{:S(2)}) async-start(), calls=%async_computation.28 | async-start | bytes 25165824 | tf_op jit(solution)/shard_map/reduce_scatter | solution.py:177
  1056.2 839.7 %reduce-scatter.47.cloned.1.call-start = ((), (), s32[]{:S(2)}) async-start(), calls=%async_computation.34 | async-start | bytes 4456448
  1061.9 893.8 %reduce-scatter.45.cloned.1.call-start = ((), (), s32[]{:S(2)}) async-start(), calls=%async_computation.33 | async-start | bytes 4456448
  1118.6 913.2 %reduce-scatter.29.cloned.1.call-start = ((), (), s32[]{:S(2)}) async-start(), calls=%async_computation.25 | async-start | bytes 4456448 | tf_op jit(solution)/shard_map/reduce_scatter | solution.py:284
  1175.1 932.8 %reduce-scatter.43.cloned.1.call-start = ((), (), s32[]{:S(2)}) async-start(), calls=%async_computation.32 | async-start | bytes 4456448
  1231.9 1057.2 %reduce-scatter.41.cloned.1.call-start = ((), (), s32[]{:S(2)}) async-start(), calls=%async_computation.31 | async-start | bytes 17825792 | tf_op jit(solution)/shard_map/reduce_scatter | solution.py:190
  1430.9 1039.2 %reduce-scatter.33.cloned.1.call-start = ((), (), s32[]{:S(2)}) async-start(), calls=%async_computation.27 | async-start | bytes 17825792 | tf_op jit(solution)/shard_map/reduce_scatter | solution.py:188
  1622.5 1028.7 %reduce-scatter.37.cloned.1.call-start = ((), (), s32[]{:S(2)}) async-start(), calls=%async_computation.29 | async-start | bytes 17825792 | tf_op jit(solution)/shard_map/reduce_scatter | solution.py:189
  1813.6 73.4 %copy-start.4 = (f32[128,2048]{1,0:T(8,128)S(1)}, f32[128,2048]{1,0:T(8,128)}, u32[]{:S(2)}) copy-start(f32[128,2048]{1,0:T(8,128)} %get-tuple-element.97) | copy-start | bytes 3145732
  1813.6 73.4 %copy-start.21 = (bf16[128,1024]{1,0:T(8,128)(2,1)S(1)}, bf16[128,1024]{1,0:T(8,128)(2,1)}, u32[]{:S(2)}) copy-start(bf16[128,1024]{1,0:T(8,128)(2,1)} %copy-done.20) | copy-start | bytes 786436
  1813.6 77.3 %copy-start.19 = (bf16[128,1024]{1,0:T(8,128)(2,1)S(1)}, bf16[128,1024]{1,0:T(8,128)(2,1)}, u32[]{:S(2)}) copy-start(bf16[128,1024]{1,0:T(8,128)(2,1)} %copy-done.18) | copy-start | bytes 786436
  (43 other events, 186.9 us)
Sparse Core Ops, SparseCore 0:
  9.5 104.4 all-gather.13
  115.6 101.7 all-gather.11
  218.9 101.7 all-gather.9
  322.1 56.8 all-gather.15
  380.4 198.8 all-gather.17
  580.7 198.8 all-gather.19
  781.1 198.8 all-gather.21
  1003.3 54.3 reduce-scatter.24
  1060.0 54.3 reduce-scatter.22
  1116.6 54.3 reduce-scatter.26
  1173.3 54.3 reduce-scatter.20
  1229.9 189.1 reduce-scatter.38
  1421.4 189.1 reduce-scatter.30
  1612.8 189.1 reduce-scatter.34
  1806.3 73.4 reduce-scatter.46
  1884.1 71.5 reduce-scatter.44
  1960.0 71.8 reduce-scatter.28
  2036.1 71.7 reduce-scatter.42
  2112.6 176.4 reduce-scatter.40
  2293.6 176.4 reduce-scatter.32
  2474.7 176.4 reduce-scatter.36
